TPU v7x, 32 devices: a whole 2x2x4 slice. The times are simulated.
32 devices in a mesh: dp: 4 (over x, core), tensor: 8 (over z, y).
Axes of the slice: x: 2, y: 2, z: 4, core: 2. Of those that a mesh axis runs over, the one named last changes fastest.
Arguments:
- attn_ctx: bfloat16 [2048, 8192], P('dp', 'tensor'), may hold values from -6 to 6
- w_out: bfloat16 [8192, 8192], P('tensor'), may hold values from -0.09375 to 0.09375
- resid: bfloat16 [2048, 8192], P(('dp', 'tensor')), may hold values from -6 to 6
- teacher_gain: bfloat16 [8192], replicated, may hold values from 0.25 to 1.75
- dest_row: int32 [2048], replicated, may hold values from 0 to 2047, as said below
- student_in: bfloat16 [2048, 4096], P('dp', 'tensor'), may hold values from -6 to 6
- student_gain: bfloat16 [4096], replicated, may hold values from 0.25 to 1.75
- w_gate: bfloat16 [4096, 14336], P('dp', 'tensor'), may hold values from -0.09375 to 0.09375
- w_up: bfloat16 [4096, 14336], P('dp', 'tensor'), may hold values from -0.09375 to 0.09375
- w_down: bfloat16 [14336, 4096], P('tensor', 'dp'), may hold values from -0.0625 to 0.0625
- proj: bfloat16 [4096, 8192], P('dp', 'tensor'), may hold values from -0.09375 to 0.09375
Outputs:
- student_out: bfloat16 [2048, 4096], P('dp', 'tensor')
- row_loss: float32 [2048], P('dp')
- residue: float32 [2048, 8192], P('dp', 'tensor')
Inputs may be any that keep to these rules, and one draw needn't show every extreme that they name: A permutation of the rows; of the 64 rows i in one aligned block of teacher rows, at most 32 have dest_row[i] in any one tile of 512 student rows, and some tile receives exactly 32 of them.
All inputs are finite; a program needn't handle non-finite values.
Results may differ from a plain program's by a relative error of at most 0.012.
Values may be sent and summed in bfloat16 or wider, within the bound.
A program may use at most 192 MiB of HBM per device.

v0:
```python
import jax
import jax.numpy as jnp
from jax import lax
from jax.sharding import PartitionSpec as P

HT = 8192


def local(
    attn_ctx,
    w_out,
    resid,
    teacher_gain,
    dest_row,
    student_in,
    student_gain,
    w_gate,
    w_up,
    w_down,
    proj,
):
    tensor_count = lax.axis_size("tensor")
    group_count = lax.axis_size("dp")
    tile_rows = attn_ctx.shape[0]
    own_rows = resid.shape[0]
    portion = attn_ctx
    summed = lax.psum_scatter(
        jnp.dot(portion, w_out, preferred_element_type=jnp.float32).astype(jnp.bfloat16),
        "tensor",
        scatter_dimension=0,
        tiled=True,
    ).astype(jnp.float32)
    teacher_hidden = resid.astype(jnp.float32) + summed
    square_mean = jnp.mean(teacher_hidden * teacher_hidden, axis=1, keepdims=True)
    teacher_final = (
        teacher_hidden * lax.rsqrt(square_mean + 1e-06) * teacher_gain.astype(jnp.float32)
    ).astype(jnp.bfloat16)
    capacity = 2 * own_rows // group_count
    source_count = group_count * tensor_count
    group_ids = (dest_row // tile_rows).reshape(source_count, own_rows)
    onehot = (group_ids[:, :, None] == jnp.arange(group_count)[None, None, :]).astype(jnp.int32)
    slot_index = jnp.sum((jnp.cumsum(onehot, 1) - onehot) * onehot, 2)
    my_source = lax.axis_index("dp") * tensor_count + lax.axis_index("tensor")
    own_groups = lax.dynamic_index_in_dim(group_ids, my_source, 0, keepdims=False)
    own_slots = lax.dynamic_index_in_dim(slot_index, my_source, 0, keepdims=False)
    target_slot = own_groups * capacity + own_slots
    selector = (target_slot[None, :] == jnp.arange(group_count * capacity)[:, None]).astype(
        jnp.bfloat16
    )
    packed = jnp.dot(selector, teacher_final, preferred_element_type=jnp.float32).astype(
        jnp.bfloat16
    )
    col_width = teacher_final.shape[1] // tensor_count
    send_blocks = packed.reshape(group_count, capacity, tensor_count, col_width).transpose(
        0, 2, 1, 3
    )
    arrived = lax.all_to_all(
        lax.all_to_all(send_blocks, "dp", split_axis=0, concat_axis=0, tiled=True),
        "tensor",
        split_axis=1,
        concat_axis=1,
        tiled=True,
    )
    flattened = arrived.reshape(source_count * capacity, col_width)
    arrival_index = (jnp.arange(source_count)[:, None] * capacity + slot_index).reshape(-1)
    inverse = jnp.zeros(dest_row.shape, jnp.int32).at[dest_row].set(arrival_index)
    own_arrivals = lax.dynamic_slice_in_dim(inverse, lax.axis_index("dp") * tile_rows, tile_rows, 0)
    target = jnp.take(flattened, own_arrivals, axis=0)
    gathered = lax.all_gather(student_in, "tensor", axis=1, tiled=True)
    x_full = gathered.astype(jnp.float32)
    student_mean = jnp.mean(x_full * x_full, axis=1, keepdims=True)
    normed = (x_full * lax.rsqrt(student_mean + 1e-05) * student_gain.astype(jnp.float32)).astype(
        jnp.bfloat16
    )

    def add_rows(portion):
        return jnp.dot(normed, portion, preferred_element_type=jnp.float32)

    gate_acts = add_rows(lax.all_gather(w_gate, "dp", axis=0, tiled=True))
    up_acts = add_rows(lax.all_gather(w_up, "dp", axis=0, tiled=True))
    hidden = (jax.nn.silu(gate_acts) * up_acts).astype(jnp.bfloat16)
    partial_sum = jnp.dot(
        hidden, lax.all_gather(w_down, "dp", axis=1, tiled=True), preferred_element_type=jnp.float32
    )
    local_cols = student_in.shape[1]
    mlp_sum = lax.psum(partial_sum.astype(jnp.bfloat16), "tensor").astype(jnp.float32)
    out_full = (x_full + mlp_sum).astype(jnp.bfloat16)
    out_local = lax.dynamic_slice_in_dim(
        out_full, lax.axis_index("tensor") * local_cols, local_cols, 1
    )
    pred = jnp.dot(
        out_full, lax.all_gather(proj, "dp", axis=0, tiled=True), preferred_element_type=jnp.float32
    )
    residue = pred - target.astype(jnp.float32)
    row_error = jnp.sum(residue * residue, axis=1)
    row_loss = lax.psum(row_error, "tensor") / HT
    return (out_local, row_loss, residue)


def solution(mesh):
    placed = (
        P("dp", "tensor"),
        P("tensor", None),
        P(("dp", "tensor"), None),
        P(),
        P(),
        P("dp", "tensor"),
        P(),
        P("dp", "tensor"),
        P("dp", "tensor"),
        P("tensor", "dp"),
        P("dp", "tensor"),
    )
    return jax.shard_map(
        local,
        mesh=mesh,
        in_specs=placed,
        out_specs=(P("dp", "tensor"), P("dp"), P("dp", "tensor")),
        check_vma=False,
    )
```

profile of v0, /device:TPU:0, one launch (start us, length us, event | category | flops | bytes accessed | tf_op | source)
XLA Modules:
  0.0 813.1 jit_solution(8429802727703756237)
XLA Ops:
  7.2 0.7 all-gather.6.cloned.1.call-update
  7.9 0.0 all-gather.8.cloned.1.call-start
  8.0 0.7 all-gather.8.cloned.1.call-update
  8.7 0.0 all-gather.12.cloned.1.call-start
  8.7 0.7 all-gather.12.cloned.1.call-update
  9.4 0.0 all-gather.10.cloned.1.call-start
  9.4 0.5 all-gather.10.cloned.1.call-update
  10.0 0.0 reduce-scatter.2.cloned.1.call-start
  10.0 16.8 %convolution_convert_fusion = bf16[512,8192]{1,0:T(8,128)(2,1)} fusion(bf16[512,1024]{1,0:T(8,128)(2,1)S(1)} %copy-done, bf16[1024,8192]{1,0:T(8,128)(2,1)} %param.12), kind=kOutput, calls=%fused_computation.5 | convolution fusion | flops 8594128896 | bytes 26214400 | tf_op jit(solution)/shard_map/dot_general | solution.py:28
  26.8 0.2 all-reduce.2.cloned.1.call-start
  27.1 0.4 copy-done.6
  27.5 59.9 %all-gather.6.cloned.1.call-done = bf16[512,4096]{1,0:T(8,128)(2,1)} async-done(((bf16[512,512]{1,0:T(8,128)(2,1)}), bf16[512,4096]{1,0:T(8,128)(2,1)}) %all-gather.6.cloned.1.call-update) | async-done | bytes 4194320 | tf_op jit(solution)/shard_map/all_gather | solution.py:69
  87.4 3.1 fusion
  90.5 90.7 %all-gather.8.cloned.1.call-done = bf16[4096,1792]{1,0:T(8,128)(2,1)} async-done(((bf16[1024,1792]{1,0:T(8,128)(2,1)}), bf16[4096,1792]{1,0:T(8,128)(2,1)}) %all-gather.8.cloned.1.call-update) | async-done | bytes 14680080 | tf_op jit(solution)/shard_map/all_gather | solution.py:79
  181.2 14.7 %fusion.11 = f32[512,1792]{1,0:T(8,128)} fusion(bf16[4096,1792]{1,0:T(8,128)(2,1)} %all-gather.8.cloned.1.call-done, bf16[512,4096]{1,0:T(8,128)(2,1)} %all-gather.6.cloned.1.call-done, f32[4096]{0:T(1024)S(1)} %convert_element_type.47, f32[512]{0:T(512)S(1)} %add_rsqrt_fusion), kind=kOutput, calls=%fused_computation.23 | convolution fusion | flops 7524581376 | bytes 22562816 | tf_op jit(solution)/shard_map/dot_general | solution.py:77
  195.8 80.9 %all-gather.12.cloned.1.call-done = bf16[1792,4096]{1,0:T(8,128)(2,1)} async-done(((bf16[1792,1024]{1,0:T(8,128)(2,1)}), bf16[1792,4096]{1,0:T(8,128)(2,1)}) %all-gather.12.cloned.1.call-update) | async-done | bytes 14680080 | tf_op jit(solution)/shard_map/all_gather | solution.py:83
  276.8 95.4 %all-gather.10.cloned.1.call-done = bf16[4096,1792]{1,0:T(8,128)(2,1)} async-done(((bf16[1024,1792]{1,0:T(8,128)(2,1)}), bf16[4096,1792]{1,0:T(8,128)(2,1)}) %all-gather.10.cloned.1.call-update) | async-done | bytes 14680080 | tf_op jit(solution)/shard_map/all_gather | solution.py:80
  372.2 28.8 %convolution_convert_fusion.2 = bf16[512,4096]{1,0:T(8,128)(2,1)} fusion(bf16[1792,4096]{1,0:T(8,128)(2,1)} %all-gather.12.cloned.1.call-done, f32[512,1792]{1,0:T(8,128)} %fusion.11, bf16[4096,1792]{1,0:T(8,128)(2,1)} %all-gather.10.cloned.1.call-done, bf16[512,4096]{1,0:T(8,128)(2,1)} %all-gather.6.cloned.1.call-done, f32[4096]{0:T(1024)S(1)} %convert_element_type.47, ...), kind=kOutput, calls=%fused_computation.11 | convolution fusion | flops 15048376320 | bytes 41437184 | tf_op jit(solution)/shard_map/dot_general | solution.py:82
  401.0 0.3 all-gather.14.cloned.1.call-start
  401.3 0.5 all-gather.14.cloned.1.call-update
  401.8 0.1 eq.30
  401.9 0.1 copy.29
  402.0 1.7 select_reduce_fusion
  403.7 0.2 add_reduce_fusion
  403.9 119.3 %reduce-scatter.2.cloned.1.call-done = bf16[64,8192]{1,0:T(8,128)(2,1)} async-done(((bf16[512,8192]{1,0:T(8,128)(2,1)}), bf16[64,8192]{1,0:T(8,128)(2,1)}) %reduce-scatter.2.cloned.1.call-update) | async-done | bytes 1048592 | tf_op jit(solution)/shard_map/reduce_scatter | solution.py:27
  523.2 1.7 multiply_reduce_fusion.1
  524.9 2.0 convolution_convert_fusion.1
  526.9 1.4 copy.35
  528.3 1.2 copy.37
  529.5 28.2 %all_to_all.10 = bf16[4,8,32,1024]{3,2,1,0:T(8,128)(2,1)S(1)} all-to-all(bf16[4,8,32,1024]{3,2,1,0:T(8,128)(2,1)S(1)} %bitcast.17), channel_id=1, replica_groups=mesh['dp'=4,'tensor'=8] {'dp'}, dimensions={0} | all-to-all | bytes 4194304 | tf_op jit(solution)/shard_map/all_to_all | solution.py:58
  557.7 1.5 copy.33
  559.1 4.3 all-to-all-start.1
  563.5 0.1 copy.30
  563.6 0.1 broadcast_add_fusion
  563.6 0.1 reshape.60
  563.7 8.3 %scatter_custom_fusion = s32[2048]{0:T(1024)S(1)} fusion(s32[2048]{0:T(1024)S(1)} %get-tuple-element.5, s32[2048]{0:T(1024)S(1)} %reshape.60, s32[]{:T(128)} %constant.62.clone.1), kind=kCustom, calls=%fused_computation.43 | custom fusion | bytes 8196 | tf_op jit(solution)/shard_map/scatter | solution.py:66
  572.0 0.1 compare_and_fusion
  572.1 64.3 %all-to-all-done.1 = bf16[4,8,32,1024]{3,2,0,1:T(8,128)(2,1)} async-done(((bf16[4,8,32,1024]{3,2,0,1:T(8,128)(2,1)}), bf16[4,8,32,1024]{3,2,0,1:T(8,128)(2,1)}, u32[]{:S(2)}, u32[]{:S(2)}) %all-to-all-start.1) | async-done | bytes 2097184 | tf_op jit(solution)/shard_map/all_to_all | solution.py:57
  636.5 1.8 copy.34
  638.3 2.8 gather_fusion
  641.1 73.8 %all-reduce.2.cloned.1.call-done = bf16[512,4096]{1,0:T(8,128)(2,1)} async-done(((bf16[512,4096]{1,0:T(8,128)(2,1)}), bf16[512,4096]{1,0:T(8,128)(2,1)}) %all-reduce.2.cloned.1.call-update) | async-done | bytes 4194320 | tf_op jit(solution)/shard_map/psum | solution.py:86
  714.9 5.0 fusion.3
  719.9 1.9 copy-done.2
  721.8 0.8 constant_dynamic-slice_fusion
  722.7 51.0 %all-gather.14.cloned.1.call-done = bf16[4096,1024]{1,0:T(8,128)(2,1)} async-done(((bf16[1024,1024]{1,0:T(8,128)(2,1)}), bf16[4096,1024]{1,0:T(8,128)(2,1)}) %all-gather.14.cloned.1.call-update) | async-done | bytes 8388624 | tf_op jit(solution)/shard_map/all_gather | solution.py:92
  773.7 10.6 %multiply_reduce_fusion = (f32[512]{0:T(512)S(1)}, f32[512,1024]{1,0:T(8,128)}) fusion(bf16[512,1024]{1,0:T(8,128)(2,1)S(1)} %copy-done.4, pred[512]{0:T(512)(128)(4,1)S(1)} %get-tuple-element.3, bf16[512,4096]{1,0:T(8,128)(2,1)} %copy-done.2, bf16[4096,1024]{1,0:T(8,128)(2,1)} %all-gather.14.cloned.1.call-done), kind=kOutput, calls=%fused_computation.14 | convolution fusion | flops 4297588224 | bytes 15731200 | tf_op jit(solution)/shard_map/dot_general | solution.py:91
  784.3 21.3 %psum.15 = f32[512]{0:T(512)S(1)} all-reduce(f32[512]{0:T(512)S(1)} %get-tuple-element.7), channel_id=1, replica_groups=mesh['dp'=4,'tensor'=8] {'tensor'}, use_global_device_ids=true, to_apply=%region_8.9 | all-reduce | flops 512 | bytes 4096 | tf_op jit(solution)/shard_map/psum | solution.py:96
  805.6 0.6 broadcast_multiply_fusion
  (24 shorter events, 0.1 us)
Async XLA Ops:
  7.2 2.9 copy-start
  7.2 80.2 %all-gather.6.cloned.1.call-start = ((), (), s32[]{:S(2)}) async-start(), calls=%async_computation.3 | async-start | bytes 4718592 | tf_op jit(solution)/shard_map/all_gather | solution.py:69
  7.9 173.3 %all-gather.8.cloned.1.call-start = ((), (), s32[]{:S(2)}) async-start(), calls=%async_computation.4 | async-start | bytes 18350080 | tf_op jit(solution)/shard_map/all_gather | solution.py:79
  8.7 268.1 %all-gather.12.cloned.1.call-start = ((), (), s32[]{:S(2)}) async-start(), calls=%async_computation.6 | async-start | bytes 18350080 | tf_op jit(solution)/shard_map/all_gather | solution.py:83
  9.4 362.8 %all-gather.10.cloned.1.call-start = ((), (), s32[]{:S(2)}) async-start(), calls=%async_computation.5 | async-start | bytes 18350080 | tf_op jit(solution)/shard_map/all_gather | solution.py:80
  10.0 513.2 %reduce-scatter.2.cloned.1.call-start = ((), (), s32[]{:S(2)}) async-start(), calls=%async_computation.9 | async-start | bytes 9437184 | tf_op jit(solution)/shard_map/reduce_scatter | solution.py:27
  26.8 0.7 copy-start.6
  26.8 688.0 %all-reduce.2.cloned.1.call-start = ((), (), s32[]{:S(2)}) async-start(), calls=%async_computation.7 | async-start | bytes 8388608 | tf_op jit(solution)/shard_map/psum | solution.py:86
  401.0 0.8 copy-start.5
  401.0 0.8 copy-start.7
  401.0 122.2 %copy-start.3 = (bf16[64,8192]{1,0:T(8,128)(2,1)S(1)}, bf16[64,8192]{1,0:T(8,128)(2,1)}, u32[]{:S(2)}) copy-start(bf16[64,8192]{1,0:T(8,128)(2,1)} %param.13) | copy-start | bytes 3145732
  401.0 372.7 %all-gather.14.cloned.1.call-start = ((), (), s32[]{:S(2)}) async-start(), calls=%async_computation.8 | async-start | bytes 10485760 | tf_op jit(solution)/shard_map/all_gather | solution.py:92
  559.1 77.3 %all-to-all-start.1 = ((bf16[4,8,32,1024]{3,2,0,1:T(8,128)(2,1)}), bf16[4,8,32,1024]{3,2,0,1:T(8,128)(2,1)}, u32[]{:S(2)}, u32[]{:S(2)}) async-start(bf16[4,8,32,1024]{3,2,0,1:T(8,128)(2,1)} %copy.33), calls=%async_computation.2 | async-start | bytes 4194304 | tf_op jit(solution)/shard_map/all_to_all | solution.py:57
  641.1 132.7 %copy-start.4 = (bf16[512,1024]{1,0:T(8,128)(2,1)S(1)}, bf16[512,1024]{1,0:T(8,128)(2,1)}, u32[]{:S(2)}) copy-start(bf16[512,1024]{1,0:T(8,128)(2,1)} %gather_fusion) | copy-start | bytes 3145732
  719.9 2.0 copy-start.2
  773.7 32.5 %copy-start.1 = (bf16[512,1024]{1,0:T(8,128)(2,1)S(1)}, bf16[512,1024]{1,0:T(8,128)(2,1)}, u32[]{:S(2)}) copy-start(bf16[512,1024]{1,0:T(8,128)(2,1)} %param.11) | copy-start | bytes 3145732
Sparse Core Ops, SparseCore 0:
  10.0 77.3 all-gather.5
  89.0 92.1 all-gather.7
  182.8 93.9 all-gather.11
  278.2 93.9 all-gather.9
  375.7 147.4 reduce-scatter.1
  526.7 188.0 all-reduce.1
  716.4 57.2 all-gather.13
where the time goes:
time: 814 us; the launch traced here: 813 us
  waiting for transfers between devices  639 us (79%)
  matrix products  72.8 us (9%)
  blocking collectives  49.5 us (6%)
  local copies, waits for them, and re-layouts  20.5 us (3%)
  between operations  14.3 us (2%)
  other arithmetic  12.4 us (2%)
    reduce_scatter x1, waiting for transfers between devices, local(): lax.psum_scatter(jnp.dot(portion, w_out, preferred_element_type=jnp.float...  119 us
    all_gather x1, waiting for transfers between devices, local(): up_acts = add_rows(lax.all_gather(w_up, 'dp', axis=0, tiled=True))  95.4 us
    all_gather x1, waiting for transfers between devices, local(): gate_acts = add_rows(lax.all_gather(w_gate, 'dp', axis=0, tiled=True))  90.7 us
    all_gather x1, waiting for transfers between devices, local(): lax.all_gather(w_down, 'dp', axis=1, tiled=True)  80.9 us
    psum x1, waiting for transfers between devices, local(): lax.psum(partial_sum.astype(jnp.bfloat16), 'tensor').astype(jnp.float32)  73.8 us
    all_to_all x1, waiting for transfers between devices, local(): lax.all_to_all(lax.all_to_all(send_blocks, 'dp', split_axis=0, concat_axi...  64.3 us
    all_gather x1, waiting for transfers between devices, local(): gathered = lax.all_gather(student_in, 'tensor', axis=1, tiled=True)  59.9 us
    all_gather x1, waiting for transfers between devices, local(): lax.all_gather(proj, 'dp', axis=0, tiled=True)  51 us
  transfers between devices with their start and end apart: 8, of which 8 were waited for; matrix products, arithmetic and copies ran while one was open for 11% of the time, Pallas kernels for 0%

commit v1 on v0

--- a/solution.py
+++ b/solution.py
@@ -1,9 +1,28 @@
+import functools
 import jax
 import jax.numpy as jnp
 from jax import lax
 from jax.sharding import PartitionSpec as P
 
 HT = 8192
+
+
+def get_squares(xx, array_dim):
+    ndev = jax.lax.axis_size("tensor")
+    wide_out = sorted(((hop_no, (hop_no + 1) % ndev) for hop_no in range(ndev)))
+    piece_now = xx
+    in_order = [piece_now]
+    c = 1
+    while c < ndev:
+        piece_now = jax.lax.ppermute(piece_now, "tensor", perm=wide_out)
+        in_order.insert(0, piece_now)
+        c += 1
+    tall = jnp.concatenate(in_order, axis=array_dim)
+    newest = jax.lax.axis_index("tensor") + 1
+    return jnp.roll(tall, newest * xx.shape[array_dim], axis=array_dim)
+
+
+advance_row = functools.partial(get_squares, array_dim=1)
 
 
 def local(
@@ -66,7 +85,7 @@
     inverse = jnp.zeros(dest_row.shape, jnp.int32).at[dest_row].set(arrival_index)
     own_arrivals = lax.dynamic_slice_in_dim(inverse, lax.axis_index("dp") * tile_rows, tile_rows, 0)
     target = jnp.take(flattened, own_arrivals, axis=0)
-    gathered = lax.all_gather(student_in, "tensor", axis=1, tiled=True)
+    gathered = advance_row(student_in)
     x_full = gathered.astype(jnp.float32)
     student_mean = jnp.mean(x_full * x_full, axis=1, keepdims=True)
     normed = (x_full * lax.rsqrt(student_mean + 1e-05) * student_gain.astype(jnp.float32)).astype(

time: 814 us -> 562 us (0.69)
  waiting for transfers between devices: 639 us -> 350 us
  blocking collectives: 49.5 us -> 70.1 us
  local copies, waits for them, and re-layouts: 20.5 us -> 30.9 us
    reduce_scatter x1, waiting for transfers between devices: 119 us -> 0.03 us  [local(): lax.psum_scatter(jnp.dot(portion, w_out, preferred_element_type=jnp.float...]
    all_gather x1, waiting for transfers between devices: 90.7 us -> 0.02 us  [local(): gate_acts = add_rows(lax.all_gather(w_gate, 'dp', axis=0, tiled=True))]
    ppermute x0 -> x7, waiting for transfers between devices: none -> 85.4 us  [get_squares(): piece_now = jax.lax.ppermute(piece_now, 'tensor', perm=wide_out)]
    all_gather x1 -> x0, waiting for transfers between devices: 59.9 us -> none  [local(): gathered = lax.all_gather(student_in, 'tensor', axis=1, tiled=True)]
    all_gather x1, waiting for transfers between devices: 51 us -> 0.01 us  [local(): lax.all_gather(proj, 'dp', axis=0, tiled=True)]
    all_gather x1, waiting for transfers between devices: 95.4 us -> 59.3 us  [local(): up_acts = add_rows(lax.all_gather(w_up, 'dp', axis=0, tiled=True))]
    psum x1, waiting for transfers between devices: 73.8 us -> 49.9 us  [local(): lax.psum(partial_sum.astype(jnp.bfloat16), 'tensor').astype(jnp.float32)]
    all_to_all x1, blocking collectives: 28.2 us -> 51 us  [local(): lax.all_to_all(send_blocks, 'dp', split_axis=0, concat_axis=0, tiled=True)]
  transfers between devices with their start and end apart: 8 -> 14, of which waited for: 8 -> 10; matrix products, arithmetic and copies ran while one was open for 11% -> 17% of each run, Pallas kernels for 0% -> 0%
where the time goes in v1:
time: 562 us; the launch traced here: 561 us
  waiting for transfers between devices  350 us (62%)
  matrix products  73 us (13%)
  blocking collectives  70.1 us (12%)
  local copies, waits for them, and re-layouts  30.9 us (5%)
  between operations  15.5 us (3%)
  other arithmetic  12.4 us (2%)
  starting transfers between devices  9.08 us (2%)
    all_gather x1, waiting for transfers between devices, local(): lax.all_gather(w_down, 'dp', axis=1, tiled=True)  95.6 us
    ppermute x7, waiting for transfers between devices, get_squares(): piece_now = jax.lax.ppermute(piece_now, 'tensor', perm=wide_out)  85.4 us
    all_gather x1, waiting for transfers between devices, local(): up_acts = add_rows(lax.all_gather(w_up, 'dp', axis=0, tiled=True))  59.3 us
    all_to_all x1, waiting for transfers between devices, local(): lax.all_to_all(lax.all_to_all(send_blocks, 'dp', split_axis=0, concat_axi...  57.3 us
    all_to_all x1, blocking collectives, local(): lax.all_to_all(send_blocks, 'dp', split_axis=0, concat_axis=0, tiled=True)  51 us
    psum x1, waiting for transfers between devices, local(): lax.psum(partial_sum.astype(jnp.bfloat16), 'tensor').astype(jnp.float32)  49.9 us
    dot_general x1, matrix products, local(): jnp.dot(hidden, lax.all_gather(w_down, 'dp', axis=1, tiled=True), preferr...  28.8 us
    psum x1, blocking collectives, local(): row_loss = lax.psum(row_error, 'tensor') / HT  19.1 us
  transfers between devices with their start and end apart: 14, of which 10 were waited for; matrix products, arithmetic and copies ran while one was open for 17% of the time, Pallas kernels for 0%

profile of v1, /device:TPU:0, one launch (start us, length us, event | category | flops | bytes accessed | tf_op | source)
XLA Modules:
  0.0 561.0 jit_solution(1530038092957225088)
XLA Ops:
  8.1 0.7 all-gather.5.cloned.1.call-update
  8.8 0.7 all-gather.7.cloned.1.call-update
  9.6 0.7 all-gather.9.cloned.1.call-update
  10.3 3.0 collective-permute-start
  13.4 15.0 %collective-permute-done = bf16[512,512]{1,0:T(8,128)(2,1)S(1)} collective-permute-done((bf16[512,512]{1,0:T(8,128)(2,1)S(1)}, bf16[512,512]{1,0:T(8,128)(2,1)S(1)}, u32[]{:S(2)}, u32[]{:S(2)}) %collective-permute-start) | collective-permute-done | bytes 524320 | tf_op jit(solution)/shard_map/ppermute | solution.py:17
  28.3 15.8 %collective-permute-done.1 = bf16[512,512]{1,0:T(8,128)(2,1)S(1)} collective-permute-done((bf16[512,512]{1,0:T(8,128)(2,1)S(1)}, bf16[512,512]{1,0:T(8,128)(2,1)S(1)}, u32[]{:S(2)}, u32[]{:S(2)}) %collective-permute-start.1) | collective-permute-done | bytes 524320 | tf_op jit(solution)/shard_map/ppermute | solution.py:17
  44.1 14.9 %collective-permute-done.2 = bf16[512,512]{1,0:T(8,128)(2,1)S(1)} collective-permute-done((bf16[512,512]{1,0:T(8,128)(2,1)S(1)}, bf16[512,512]{1,0:T(8,128)(2,1)S(1)}, u32[]{:S(2)}, u32[]{:S(2)}) %collective-permute-start.2) | collective-permute-done | bytes 524320 | tf_op jit(solution)/shard_map/ppermute | solution.py:17
  59.0 14.1 %collective-permute-done.3 = bf16[512,512]{1,0:T(8,128)(2,1)S(1)} collective-permute-done((bf16[512,512]{1,0:T(8,128)(2,1)S(1)}, bf16[512,512]{1,0:T(8,128)(2,1)S(1)}, u32[]{:S(2)}, u32[]{:S(2)}) %collective-permute-start.3) | collective-permute-done | bytes 524320 | tf_op jit(solution)/shard_map/ppermute | solution.py:17
  73.1 0.8 copy-done.5
  73.9 13.2 %collective-permute-done.4 = bf16[512,512]{1,0:T(8,128)(2,1)S(1)} collective-permute-done((bf16[512,512]{1,0:T(8,128)(2,1)S(1)}, bf16[512,512]{1,0:T(8,128)(2,1)S(1)}, u32[]{:S(2)}, u32[]{:S(2)}) %collective-permute-start.4) | collective-permute-done | bytes 524320 | tf_op jit(solution)/shard_map/ppermute | solution.py:17
  87.1 0.8 copy-done.7
  87.9 12.5 %collective-permute-done.5 = bf16[512,512]{1,0:T(8,128)(2,1)} collective-permute-done((bf16[512,512]{1,0:T(8,128)(2,1)S(1)}, bf16[512,512]{1,0:T(8,128)(2,1)}, u32[]{:S(2)}, u32[]{:S(2)}) %collective-permute-start.5) | collective-permute-done | bytes 524320 | tf_op jit(solution)/shard_map/ppermute | solution.py:17
  100.4 16.8 %convolution_convert_fusion = bf16[512,8192]{1,0:T(8,128)(2,1)} fusion(bf16[512,1024]{1,0:T(8,128)(2,1)S(1)} %copy-done, bf16[1024,8192]{1,0:T(8,128)(2,1)} %param.12), kind=kOutput, calls=%fused_computation.5 | convolution fusion | flops 8594128896 | bytes 26214400 | tf_op jit(solution)/shard_map/dot_general | solution.py:47
  117.3 0.2 all-reduce.2.cloned.1.call-start
  117.5 0.4 copy-done.11
  117.9 1.2 constant_dynamic-update-slice_fusion.15
  119.1 1.3 constant_dynamic-update-slice_fusion.14
  120.9 1.2 constant_dynamic-update-slice_fusion.7
  122.1 1.3 constant_dynamic-update-slice_fusion.6
  123.8 4.1 copy-done.2
  127.9 0.9 fusion
  128.8 14.6 %fusion.13 = f32[512,1792]{1,0:T(8,128)} fusion(bf16[4096,1792]{1,0:T(8,128)(2,1)} %all-gather.5.cloned.1.call-done, f32[4096]{0:T(1024)S(1)} %convert_element_type.47, f32[512]{0:T(512)S(1)} %add_rsqrt_fusion, bf16[512,8192]{1,0:T(8,128)(2,1)} %copy-done.2, s32[]{:T(128)S(6)} %select_n.42), kind=kOutput, calls=%fused_computation.27 | convolution fusion | flops 7524581376 | bytes 22562820 | tf_op jit(solution)/shard_map/dot_general | solution.py:96
  143.4 59.3 %all-gather.7.cloned.1.call-done = bf16[4096,1792]{1,0:T(8,128)(2,1)} async-done(((bf16[1024,1792]{1,0:T(8,128)(2,1)}), bf16[4096,1792]{1,0:T(8,128)(2,1)}) %all-gather.7.cloned.1.call-update) | async-done | bytes 14680080 | tf_op jit(solution)/shard_map/all_gather | solution.py:99
  202.7 95.6 %all-gather.9.cloned.1.call-done = bf16[1792,4096]{1,0:T(8,128)(2,1)} async-done(((bf16[1792,1024]{1,0:T(8,128)(2,1)}), bf16[1792,4096]{1,0:T(8,128)(2,1)}) %all-gather.9.cloned.1.call-update) | async-done | bytes 14680080 | tf_op jit(solution)/shard_map/all_gather | solution.py:102
  298.3 28.8 %convolution_convert_fusion.2 = bf16[512,4096]{1,0:T(8,128)(2,1)} fusion(bf16[1792,4096]{1,0:T(8,128)(2,1)} %all-gather.9.cloned.1.call-done, f32[512,1792]{1,0:T(8,128)} %fusion.13, bf16[4096,1792]{1,0:T(8,128)(2,1)} %all-gather.7.cloned.1.call-done, f32[4096]{0:T(1024)S(1)} %convert_element_type.47, f32[512]{0:T(512)S(1)} %add_rsqrt_fusion, ...), kind=kOutput, calls=%fused_computation.11 | convolution fusion | flops 15048376320 | bytes 41437188 | tf_op jit(solution)/shard_map/dot_general | solution.py:101
  327.2 0.3 all-gather.11.cloned.1.call-start
  327.4 0.3 all-gather.11.cloned.1.call-update
  327.8 0.1 copy.29
  327.9 1.7 select_reduce_fusion
  329.7 0.2 add_reduce_fusion
  329.9 1.7 multiply_reduce_fusion.1
  331.6 2.1 convolution_convert_fusion.1
  333.7 1.4 copy.35
  335.1 1.2 copy.37
  336.3 51.0 %all_to_all.10 = bf16[4,8,32,1024]{3,2,1,0:T(8,128)(2,1)S(1)} all-to-all(bf16[4,8,32,1024]{3,2,1,0:T(8,128)(2,1)S(1)} %bitcast.17), channel_id=1, replica_groups=mesh['dp'=4,'tensor'=8] {'dp'}, dimensions={0} | all-to-all | bytes 4194304 | tf_op jit(solution)/shard_map/all_to_all | solution.py:77
  387.2 1.5 copy.33
  388.7 5.4 all-to-all-start.1
  394.3 8.3 %scatter_custom_fusion = s32[2048]{0:T(1024)S(1)} fusion(s32[2048]{0:T(1024)S(1)} %get-tuple-element.5, s32[2048]{0:T(1024)S(1)} %reshape.60, s32[]{:T(128)} %constant.77.clone.1), kind=kCustom, calls=%fused_computation.59 | custom fusion | bytes 8196 | tf_op jit(solution)/shard_map/scatter | solution.py:85
  402.6 0.1 compare_and_fusion
  402.7 57.3 %all-to-all-done.1 = bf16[4,8,32,1024]{3,2,0,1:T(8,128)(2,1)} async-done(((bf16[4,8,32,1024]{3,2,0,1:T(8,128)(2,1)}), bf16[4,8,32,1024]{3,2,0,1:T(8,128)(2,1)}, u32[]{:S(2)}, u32[]{:S(2)}) %all-to-all-start.1) | async-done | bytes 2097184 | tf_op jit(solution)/shard_map/all_to_all | solution.py:76
  460.0 1.8 copy.34
  461.8 2.8 gather_fusion
  464.6 49.9 %all-reduce.2.cloned.1.call-done = bf16[512,4096]{1,0:T(8,128)(2,1)} async-done(((bf16[512,4096]{1,0:T(8,128)(2,1)}), bf16[512,4096]{1,0:T(8,128)(2,1)}) %all-reduce.2.cloned.1.call-update) | async-done | bytes 4194320 | tf_op jit(solution)/shard_map/psum | solution.py:105
  514.5 7.2 %fusion.3 = bf16[512,4096]{1,0:T(8,128)(2,1)} fusion(bf16[512,4096]{1,0:T(8,128)(2,1)} %all-reduce.2.cloned.1.call-done, bf16[512,8192]{1,0:T(8,128)(2,1)} %copy-done.2, s32[]{:T(128)S(6)} %select_n.42), kind=kLoop, calls=%fused_computation.10 | loop fusion | flops 8388608 | bytes 12582916 | tf_op jit(solution)/shard_map/convert_element_type | solution.py:106
  521.7 10.6 %multiply_reduce_fusion = (f32[512]{0:T(512)S(1)}, f32[512,1024]{1,0:T(8,128)}) fusion(bf16[512,1024]{1,0:T(8,128)(2,1)S(1)} %copy-done.9, pred[512]{0:T(512)(128)(4,1)S(1)} %get-tuple-element.3, bf16[512,4096]{1,0:T(8,128)(2,1)} %fusion.3, bf16[4096,1024]{1,0:T(8,128)(2,1)} %all-gather.11.cloned.1.call-done), kind=kOutput, calls=%fused_computation.14 | convolution fusion | flops 4297588224 | bytes 15731200 | tf_op jit(solution)/shard_map/dot_general | solution.py:110
  532.3 19.1 %psum.15 = f32[512]{0:T(512)S(1)} all-reduce(f32[512]{0:T(512)S(1)} %get-tuple-element.7), channel_id=1, replica_groups=mesh['dp'=4,'tensor'=8] {'tensor'}, use_global_device_ids=true, to_apply=%region_8.9 | all-reduce | flops 512 | bytes 4096 | tf_op jit(solution)/shard_map/psum | solution.py:115
  551.4 0.6 broadcast_multiply_fusion
  552.0 1.9 constant_dynamic-slice_fusion
  (61 shorter events, 1.5 us)
Async XLA Ops:
  8.0 92.4 %copy-start = (bf16[512,1024]{1,0:T(8,128)(2,1)S(1)}, bf16[512,1024]{1,0:T(8,128)(2,1)}, u32[]{:S(2)}) copy-start(bf16[512,1024]{1,0:T(8,128)(2,1)} %param.11) | copy-start | bytes 3145732
  8.0 2.3 copy-start.4
  8.0 120.8 %all-gather.5.cloned.1.call-start = ((), (), s32[]{:S(2)}) async-start(), calls=%async_computation.3 | async-start | bytes 18350080 | tf_op jit(solution)/shard_map/all_gather | solution.py:98
  8.8 194.0 %all-gather.7.cloned.1.call-start = ((), (), s32[]{:S(2)}) async-start(), calls=%async_computation.4 | async-start | bytes 18350080 | tf_op jit(solution)/shard_map/all_gather | solution.py:99
  9.5 288.8 %all-gather.9.cloned.1.call-start = ((), (), s32[]{:S(2)}) async-start(), calls=%async_computation.5 | async-start | bytes 18350080 | tf_op jit(solution)/shard_map/all_gather | solution.py:102
  10.2 319.6 %reduce-scatter.2.cloned.1.call-start = ((), (), s32[]{:S(2)}) async-start(), calls=%async_computation.8 | async-start | bytes 9437184 | tf_op jit(solution)/shard_map/reduce_scatter | solution.py:46
  10.3 18.0 %collective-permute-start = (bf16[512,512]{1,0:T(8,128)(2,1)S(1)}, bf16[512,512]{1,0:T(8,128)(2,1)S(1)}, u32[]{:S(2)}, u32[]{:S(2)}) collective-permute-start(bf16[512,512]{1,0:T(8,128)(2,1)S(1)} %copy-done.4), channel_id=1, source_target_pairs={{0,1},{1,2},{2,3},{3,4},{4,5},{5,6},{6,7},{7,0},{8,9},{9,10},{10,1... | collective-permute-start | bytes 1572872 | tf_op jit(solution)/shard_map/ppermute | solution.py:17
  28.3 15.8 %collective-permute-start.1 = (bf16[512,512]{1,0:T(8,128)(2,1)S(1)}, bf16[512,512]{1,0:T(8,128)(2,1)S(1)}, u32[]{:S(2)}, u32[]{:S(2)}) collective-permute-start(bf16[512,512]{1,0:T(8,128)(2,1)S(1)} %collective-permute-done), channel_id=1, source_target_pairs={{0,1},{1,2},{2,3},{3,4},{4,5},{5,6},{6,7},{7,0},{8,9},{9,10},{10,1... | collective-permute-start | bytes 1572872 | tf_op jit(solution)/shard_map/ppermute | solution.py:17
  44.1 14.9 %collective-permute-start.2 = (bf16[512,512]{1,0:T(8,128)(2,1)S(1)}, bf16[512,512]{1,0:T(8,128)(2,1)S(1)}, u32[]{:S(2)}, u32[]{:S(2)}) collective-permute-start(bf16[512,512]{1,0:T(8,128)(2,1)S(1)} %collective-permute-done.1), channel_id=1, source_target_pairs={{0,1},{1,2},{2,3},{3,4},{4,5},{5,6},{6,7},{7,0},{8,9},{9,10},{10,1... | collective-permute-start | bytes 1572872 | tf_op jit(solution)/shard_map/ppermute | solution.py:17
  59.0 14.1 %collective-permute-start.3 = (bf16[512,512]{1,0:T(8,128)(2,1)S(1)}, bf16[512,512]{1,0:T(8,128)(2,1)S(1)}, u32[]{:S(2)}, u32[]{:S(2)}) collective-permute-start(bf16[512,512]{1,0:T(8,128)(2,1)S(1)} %collective-permute-done.2), channel_id=1, source_target_pairs={{0,1},{1,2},{2,3},{3,4},{4,5},{5,6},{6,7},{7,0},{8,9},{9,10},{10,1... | collective-permute-start | bytes 1572872 | tf_op jit(solution)/shard_map/ppermute | solution.py:17
  73.1 0.8 copy-start.5
  73.9 13.2 %collective-permute-start.4 = (bf16[512,512]{1,0:T(8,128)(2,1)S(1)}, bf16[512,512]{1,0:T(8,128)(2,1)S(1)}, u32[]{:S(2)}, u32[]{:S(2)}) collective-permute-start(bf16[512,512]{1,0:T(8,128)(2,1)S(1)} %collective-permute-done.3), channel_id=1, source_target_pairs={{0,1},{1,2},{2,3},{3,4},{4,5},{5,6},{6,7},{7,0},{8,9},{9,10},{10,1... | collective-permute-start | bytes 1572872 | tf_op jit(solution)/shard_map/ppermute | solution.py:17
  87.1 0.8 copy-start.7
  87.9 12.5 %collective-permute-start.5 = (bf16[512,512]{1,0:T(8,128)(2,1)S(1)}, bf16[512,512]{1,0:T(8,128)(2,1)}, u32[]{:S(2)}, u32[]{:S(2)}) collective-permute-start(bf16[512,512]{1,0:T(8,128)(2,1)S(1)} %collective-permute-done.4), channel_id=1, source_target_pairs={{0,1},{1,2},{2,3},{3,4},{4,5},{5,6},{6,7},{7,0},{8,9},{9,10},{10,1... | collective-permute-start | bytes 1572872 | tf_op jit(solution)/shard_map/ppermute | solution.py:17
  100.4 17.6 %collective-permute-start.6 = (bf16[512,512]{1,0:T(8,128)(2,1)}, bf16[512,512]{1,0:T(8,128)(2,1)}, u32[]{:S(2)}, u32[]{:S(2)}) collective-permute-start(bf16[512,512]{1,0:T(8,128)(2,1)} %collective-permute-done.5), channel_id=1, source_target_pairs={{0,1},{1,2},{2,3},{3,4},{4,5},{5,6},{6,7},{7,0},{8,9},{9,10},{10,1... | collective-permute-start | bytes 1572872 | tf_op jit(solution)/shard_map/ppermute | solution.py:17
  117.2 0.7 copy-start.11
  117.2 3.2 copy-start.8
  117.2 3.3 copy-start.6
  117.3 397.2 %all-reduce.2.cloned.1.call-start = ((), (), s32[]{:S(2)}) async-start(), calls=%async_computation.6 | async-start | bytes 8388608 | tf_op jit(solution)/shard_map/psum | solution.py:105
  123.8 4.1 copy-start.2
  298.3 29.4 %copy-start.12 = (s32[2048]{0:T(1024)S(1)}, s32[2048]{0:T(1024)}, u32[]{:S(2)}) copy-start(s32[2048]{0:T(1024)} %param.15) | copy-start | bytes 24580
  298.3 29.6 %copy-start.10 = (bf16[8192]{0:T(1024)(128)(2,1)S(1)}, bf16[8192]{0:T(1024)(128)(2,1)}, u32[]{:S(2)}) copy-start(bf16[8192]{0:T(1024)(128)(2,1)} %param.14) | copy-start | bytes 49156
  298.3 31.6 %copy-start.3 = (bf16[64,8192]{1,0:T(8,128)(2,1)S(1)}, bf16[64,8192]{1,0:T(8,128)(2,1)}, u32[]{:S(2)}) copy-start(bf16[64,8192]{1,0:T(8,128)(2,1)} %param.13) | copy-start | bytes 3145732
  327.2 194.5 %all-gather.11.cloned.1.call-start = ((), (), s32[]{:S(2)}) async-start(), calls=%async_computation.7 | async-start | bytes 10485760 | tf_op jit(solution)/shard_map/all_gather | solution.py:111
  388.7 71.3 %all-to-all-start.1 = ((bf16[4,8,32,1024]{3,2,0,1:T(8,128)(2,1)}), bf16[4,8,32,1024]{3,2,0,1:T(8,128)(2,1)}, u32[]{:S(2)}, u32[]{:S(2)}) async-start(bf16[4,8,32,1024]{3,2,0,1:T(8,128)(2,1)} %copy.33), calls=%async_computation.2 | async-start | bytes 4194304 | tf_op jit(solution)/shard_map/all_to_all | solution.py:76
  464.6 57.1 %copy-start.9 = (bf16[512,1024]{1,0:T(8,128)(2,1)S(1)}, bf16[512,1024]{1,0:T(8,128)(2,1)}, u32[]{:S(2)}) copy-start(bf16[512,1024]{1,0:T(8,128)(2,1)} %gather_fusion) | copy-start | bytes 3145732
  521.7 32.2 %copy-start.1 = (bf16[512,1024]{1,0:T(8,128)(2,1)S(1)}, bf16[512,1024]{1,0:T(8,128)(2,1)}, u32[]{:S(2)}) copy-start(bf16[512,1024]{1,0:T(8,128)(2,1)} %param.11) | copy-start | bytes 3145732
Sparse Core Ops, SparseCore 0:
  10.4 96.6 all-gather.4
  108.7 93.9 all-gather.6
  204.3 93.9 all-gather.8
  329.2 80.7 all-gather.10
Sparse Core Ops, SparseCore 1:
  117.3 148.0 reduce-scatter.1
  327.2 187.2 all-reduce.1
